TPU v7x, 32 devices: a whole 2x2x4 slice. The times are simulated.
32 devices in a mesh: dp: 2 (over x), pz: 4 (over z), py: 4 (over y, core).
Axes of the slice: x: 2, y: 2, z: 4, core: 2. Of those that a mesh axis runs over, the one named last changes fastest.
Arguments:
- rho_re: float32 [64, 64, 64, 64], P('dp', None, 'py', 'pz'), parts along dimension 0
- rho_im: float32 [64, 64, 64, 64], P('dp', None, 'py', 'pz'), parts along dimension 0
- g_re: float32 [64, 64, 64], P('py', 'pz')
- g_im: float32 [64, 64, 64], P('py', 'pz')
Outputs:
- output 1: float32 [64, 64, 64, 64], P('dp', None, 'py', 'pz'), parts along dimension 0
- output 2: float32 [64, 64, 64, 64], P('dp', None, 'py', 'pz'), parts along dimension 0
- output 3: float32 [64, 64, 64, 64], P('dp', 'py', 'pz'), parts along dimension 0
- output 4: float32 [64, 64, 64, 64], P('dp', 'py', 'pz'), parts along dimension 0
There are 2 independent parts. A program takes and returns all parts, laid end to end along the dimension named above; an argument that names none is the same for every part.
All inputs are finite; a program needn't handle non-finite values.
Results may differ from a plain program's by a relative error of at most 0.001.
Values sent between devices are 32-bit elements.
A program may use at most 1 GiB of HBM per device.

v0:
```python
import jax
import jax.numpy as jnp
from jax import lax
from jax.sharding import PartitionSpec as P


def regroup(volume, axis_name, split_dim, concat_dim):
    halves = jnp.stack([jnp.real(volume), jnp.imag(volume)])
    arrived = lax.all_to_all(halves, axis_name, split_dim + 1, concat_dim + 1, tiled=True)
    return lax.complex(arrived[0], arrived[1])


def solution(mesh):
    def local_solve(rho_re, rho_im, g_re, g_im):
        volume = jnp.fft.fft(lax.complex(rho_re, rho_im), axis=1, norm="ortho")
        volume = regroup(volume, "py", 1, 2)
        volume = jnp.fft.fft(volume, axis=2, norm="ortho")
        volume = regroup(volume, "pz", 2, 3)
        spectrum = jnp.fft.fft(volume, axis=3, norm="ortho") * lax.complex(g_re, g_im)
        volume = jnp.fft.ifft(spectrum, axis=3, norm="ortho")
        volume = regroup(volume, "pz", 3, 2)
        volume = jnp.fft.ifft(volume, axis=2, norm="ortho")
        volume = regroup(volume, "py", 2, 1)
        volume = jnp.fft.ifft(volume, axis=1, norm="ortho")
        return jnp.real(volume), jnp.imag(volume), jnp.real(spectrum), jnp.imag(spectrum)

    space_layout = P("dp", None, "py", "pz")
    wave_layout = P("dp", "py", "pz", None)
    green_layout = P("py", "pz", None)
    return jax.shard_map(local_solve, mesh=mesh,
                         in_specs=(space_layout, space_layout, green_layout, green_layout),
                         out_specs=(space_layout, space_layout, wave_layout, wave_layout),
                         check_vma=False)
```

profile of v0, /device:TPU:0, one launch (start us, length us, event | category | flops | bytes accessed | tf_op | source)
XLA Modules:
  0.0 850.0 jit_solution(3536177282030095507)
XLA Ops:
  29.2 16.2 %copy.66 = f32[2,32,64,16,16]{1,4,3,0,2:T(8,128)} copy(f32[2,32,64,16,16]{2,1,4,3,0:T(8,128)} %pad_maximum_fusion) | data formatting | bytes 8388608 | tf_op jit(solution)/shard_map/stack | solution.py:8
  45.4 11.4 %reshape.98 = f32[4,1,262144]{2,1,0:T(1,128)} reshape(f32[64,2,16,16,32]{4,3,2,1,0:T(8,128)} %bitcast.229) | data formatting | bytes 8388608
  56.8 54.6 %all_to_all.56 = f32[4,1,262144]{2,1,0:T(1,128)} all-to-all(f32[4,1,262144]{2,1,0:T(1,128)} %reshape.98), channel_id=1, replica_groups=mesh['dp'=2,'pz'=4,'py'=4] {'py'}, dimensions={0} | all-to-all | bytes 8388608 | tf_op jit(solution)/shard_map/all_to_all | solution.py:9
  112.0 15.3 %reduce.6 = f32[4,262144]{1,0:T(4,128)} reduce(f32[4,1,262144]{2,1,0:T(1,128)} %all_to_all.56, f32[]{:T(128)} %broadcast.228), dimensions={1}, to_apply=%all_to_all.40.reduce_sub_computation | reduce | bytes 8388612 | tf_op jit(solution)/shard_map/all_to_all | solution.py:9
  127.3 13.7 %reshape.99 = f32[64,2,16,16,32]{4,3,2,1,0:T(8,128)} reshape(f32[4,262144]{1,0:T(4,128)} %reduce.6) | data formatting | bytes 8388608
  203.4 16.2 %copy.72 = f32[2,32,16,64,16]{1,4,2,0,3:T(8,128)} copy(f32[2,32,16,64,16]{3,1,4,2,0:T(8,128)} %pad_maximum_fusion.1) | data formatting | bytes 8388608 | tf_op jit(solution)/shard_map/stack | solution.py:8
  219.6 11.4 %reshape.100 = f32[4,1,262144]{2,1,0:T(1,128)} reshape(f32[64,2,16,16,32]{4,3,2,1,0:T(8,128)} %bitcast.230) | data formatting | bytes 8388608
  236.6 93.1 %all-to-all-done.1 = f32[4,1,262144]{2,1,0:T(1,128)} async-done(((f32[4,1,262144]{2,1,0:T(1,128)}), f32[4,1,262144]{2,1,0:T(1,128)}, u32[]{:S(2)}, u32[]{:S(2)}) %all-to-all-start.1) | async-done | bytes 4194336 | tf_op jit(solution)/shard_map/all_to_all | solution.py:9
  329.7 15.3 %reduce.7 = f32[4,262144]{1,0:T(4,128)} reduce(f32[4,1,262144]{2,1,0:T(1,128)} %all-to-all-done.1, f32[]{:T(128)} %broadcast.228), dimensions={1}, to_apply=%all_to_all.43.reduce_sub_computation | reduce | bytes 8388612 | tf_op jit(solution)/shard_map/all_to_all | solution.py:9
  345.0 13.7 %reshape.101 = f32[64,2,16,16,32]{4,3,2,1,0:T(8,128)} reshape(f32[4,262144]{1,0:T(4,128)} %reduce.7) | data formatting | bytes 8388608
  380.7 14.0 %fusion = f32[32,16,16,64]{3,0,2,1:T(8,128)S(1)} fusion(f32[32,16,16,64]{0,3,2,1:T(8,128)S(1)} %bitcast.225, f32[32,16,16,64]{0,3,2,1:T(8,128)S(1)} %bitcast.227), kind=kOutput, calls=%fused_computation.4 | convolution fusion | flops 403193856 | bytes 6291456 | tf_op jit(solution)/shard_map/jit(fft) | solution.py:19
  394.7 14.9 %convolution_subtract_fusion = f32[32,16,16,64]{3,0,2,1:T(8,128)} fusion(f32[32,16,16,64]{3,0,2,1:T(8,128)S(1)} %fusion, f32[32,16,16,64]{0,3,2,1:T(8,128)S(1)} %bitcast.228), kind=kOutput, calls=%fused_computation.72 | convolution fusion | flops 403197952 | bytes 6291456 | tf_op jit(solution)/shard_map/jit(fft) | solution.py:19
  409.6 15.7 %multiply_add_fusion.6 = (f32[32,16,16,64]{3,0,2,1:T(8,128)S(1)}, f32[32,16,16,64]{3,0,2,1:T(8,128)S(1)}) fusion(f32[16,16,64]{2,1,0:T(8,128)S(1)} %copy-done.11, f32[16,16,64]{2,1,0:T(8,128)S(1)} %copy-done.12, f32[32,16,16,64]{3,0,2,1:T(8,128)} %convolution_subtract_fusion, f32[32,16,16,64]{3,0,2,1:T(8,128)S(1)} %fusion, f32[32,16,16,64]{0,3,2,1:T(8,128)S(1)} %bitcast.226), kind=kOutput, calls=%fused_computation.61 | convolution fusion | flops 409489408 | bytes 10616832 | tf_op jit(solution)/shard_map/jit(fft) | solution.py:19
  442.6 16.2 %copy.79 = f32[2,32,16,16,64]{1,3,2,0,4:T(8,128)} copy(f32[2,32,16,16,64]{4,1,3,2,0:T(8,128)} %pad_maximum_fusion.2) | data formatting | bytes 8388608 | tf_op jit(solution)/shard_map/stack | solution.py:8
  458.8 11.4 %reshape.102 = f32[4,1,262144]{2,1,0:T(1,128)} reshape(f32[64,2,16,16,32]{4,3,2,1,0:T(8,128)} %bitcast.231) | data formatting | bytes 8388608
  470.2 98.3 %all_to_all.57 = f32[4,1,262144]{2,1,0:T(1,128)} all-to-all(f32[4,1,262144]{2,1,0:T(1,128)} %reshape.102), channel_id=1, replica_groups=mesh['dp'=2,'pz'=4,'py'=4] {'pz'}, dimensions={0} | all-to-all | bytes 8388608 | tf_op jit(solution)/shard_map/all_to_all | solution.py:9
  568.5 15.3 %reduce.8 = f32[4,262144]{1,0:T(4,128)} reduce(f32[4,1,262144]{2,1,0:T(1,128)} %all_to_all.57, f32[]{:T(128)} %broadcast.228), dimensions={1}, to_apply=%all_to_all.46.reduce_sub_computation | reduce | bytes 8388612 | tf_op jit(solution)/shard_map/all_to_all | solution.py:9
  583.7 13.7 %reshape.103 = f32[64,2,16,16,32]{4,3,2,1,0:T(8,128)} reshape(f32[4,262144]{1,0:T(4,128)} %reduce.8) | data formatting | bytes 8388608
  597.5 15.6 %copy.80 = f32[2,32,16,16,64]{1,4,3,2,0:T(8,128)S(1)} copy(f32[2,32,16,16,64]{1,3,2,0,4:T(8,128)} %bitcast.235) | data formatting | bytes 8388608 | tf_op jit(solution)/shard_map/all_to_all | solution.py:9
  670.5 16.2 %copy.85 = f32[2,32,16,64,16]{1,4,2,0,3:T(8,128)} copy(f32[2,32,16,64,16]{3,1,4,2,0:T(8,128)} %pad_maximum_fusion.3) | data formatting | bytes 8388608 | tf_op jit(solution)/shard_map/stack | solution.py:8
  686.7 11.6 %reshape.104 = f32[4,1,262144]{2,1,0:T(1,128)} reshape(f32[64,2,16,16,32]{4,3,2,1,0:T(8,128)} %bitcast.232) | data formatting | bytes 8388608
  714.4 36.6 %all-to-all-done.3 = f32[4,1,262144]{2,1,0:T(1,128)} async-done(((f32[4,1,262144]{2,1,0:T(1,128)}), f32[4,1,262144]{2,1,0:T(1,128)}, u32[]{:S(2)}, u32[]{:S(2)}) %all-to-all-start.3) | async-done | bytes 4194336 | tf_op jit(solution)/shard_map/all_to_all | solution.py:9
  751.0 15.7 %reduce.9 = f32[4,262144]{1,0:T(4,128)} reduce(f32[4,1,262144]{2,1,0:T(1,128)} %all-to-all-done.3, f32[]{:T(128)} %broadcast.228), dimensions={1}, to_apply=%all_to_all.49.reduce_sub_computation | reduce | bytes 8388612 | tf_op jit(solution)/shard_map/all_to_all | solution.py:9
  766.8 13.7 %reshape.105 = f32[64,2,16,16,32]{4,3,2,1,0:T(8,128)} reshape(f32[4,262144]{1,0:T(4,128)} %reduce.9) | data formatting | bytes 8388608
  (74 shorter events, 278.8 us)
Async XLA Ops:
  4.9 6.3 copy-start.9
  11.2 6.5 copy-start.10
  183.6 7.4 copy-start.3
  191.0 3.7 copy-start.4
  231.0 98.7 %all-to-all-start.1 = ((f32[4,1,262144]{2,1,0:T(1,128)}), f32[4,1,262144]{2,1,0:T(1,128)}, u32[]{:S(2)}, u32[]{:S(2)}) async-start(f32[4,1,262144]{2,1,0:T(1,128)} %reshape.100), calls=%async_computation.1 | async-start | bytes 8388608 | tf_op jit(solution)/shard_map/all_to_all | solution.py:9
  394.6 15.0 %copy-start.11 = (f32[16,16,64]{2,1,0:T(8,128)S(1)}, f32[16,16,64]{2,1,0:T(8,128)}, u32[]{:S(2)}) copy-start(f32[16,16,64]{2,1,0:T(8,128)} %param.21) | copy-start | bytes 196612
  394.7 15.0 %copy-start.12 = (f32[16,16,64]{2,1,0:T(8,128)S(1)}, f32[16,16,64]{2,1,0:T(8,128)}, u32[]{:S(2)}) copy-start(f32[16,16,64]{2,1,0:T(8,128)} %param.20) | copy-start | bytes 196612
  425.4 3.7 copy-start
  425.4 7.4 copy-start.1
  649.7 7.6 copy-start.5
  657.3 3.8 copy-start.8
  698.3 52.7 %all-to-all-start.3 = ((f32[4,1,262144]{2,1,0:T(1,128)}), f32[4,1,262144]{2,1,0:T(1,128)}, u32[]{:S(2)}, u32[]{:S(2)}) async-start(f32[4,1,262144]{2,1,0:T(1,128)} %reshape.104), calls=%async_computation.3 | async-start | bytes 8388608 | tf_op jit(solution)/shard_map/all_to_all | solution.py:9
  703.2 6.8 copy-start.2
  824.4 7.6 copy-start.6
  831.9 3.8 copy-start.7
where the time goes:
time: 861 us; the launch traced here: 850 us
  local copies, waits for them, and re-layouts  347 us (40%)
  blocking collectives  153 us (18%)
  waiting for transfers between devices  130 us (15%)
  matrix products  126 us (15%)
  other arithmetic  83.2 us (10%)
  starting transfers between devices  10.5 us (1%)
    all_to_all x2, blocking collectives, regroup(): lax.all_to_all(halves, axis_name, split_dim + 1, concat_dim + 1, tiled=True)  153 us
    all_to_all x2, waiting for transfers between devices, regroup(): lax.all_to_all(halves, axis_name, split_dim + 1, concat_dim + 1, tiled=True)  130 us
    unnamed x38, local copies, waits for them, and re-layouts  121 us
    slice x12, local copies, waits for them, and re-layouts, regroup(): return lax.complex(arrived[0], arrived[1])  80.7 us
    another operation x4, local copies, waits for them, and re-layouts, regroup(): halves = jnp.stack([jnp.real(volume), jnp.imag(volume)])  64.8 us
    all_to_all x4, other arithmetic, regroup(): lax.all_to_all(halves, axis_name, split_dim + 1, concat_dim + 1, tiled=True)  61.5 us
    another operation x3, matrix products, local_solve(): jnp.fft.fft(volume, axis=3, norm='ortho') * lax.complex(g_re, g_im)  44.6 us
    squeeze x6, local copies, waits for them, and re-layouts, regroup(): return lax.complex(arrived[0], arrived[1])  44.3 us
  transfers between devices with their start and end apart: 2, of which 2 were waited for; matrix products, arithmetic and copies ran while one was open for 1% of the time, Pallas kernels for 0%

commit v1 on v0

v1 whole, which is shorter than its diff:
```python
import functools

import jax
import jax.numpy as jnp
import numpy as np
from jax import lax
from jax.experimental import pallas as pl
from jax.experimental.pallas import tpu as pltpu
from jax.sharding import PartitionSpec as P

GRID = 64
SIDE = 4
BLOCK = 16
GROUP = 8
HALF = 8
HIGHEST = lax.Precision.HIGHEST
MESH = pl.DeviceIdType.MESH


def rotation(left, right, sign):
    angle = 2.0 * np.pi * (np.outer(left, right) % GRID) / GRID
    return np.cos(angle), sign * np.sin(angle)


def dft_matrix(rows_in, rows_out, sign, scale):
    cos, sin = rotation(rows_in, rows_out, sign)
    return np.block([[cos, sin], [-sin, cos]]) * scale


def tables():
    points = np.arange(GRID)
    kx = np.array([[[BLOCK * j + HALF * h + k for k in range(HALF)] for j in range(SIDE)] for h in range(2)])
    order = np.stack([kx, kx + GRID], axis=2).reshape(-1)
    first = dft_matrix(points, points, -1, 1.0 / 64).T[order]
    last = dft_matrix(points, points, 1, 1.0 / 8)[order]
    along_z = dft_matrix(points, points, -1, 1.0 / 8)
    back_z = dft_matrix(points, points, 1, 1.0 / 64)
    return [np.asarray(t, np.float32) for t in (first, along_z, back_z, last)]


def dft4(x):
    (a, b), (c, d), (e, f), (g, h) = x
    t0r, t0i, t1r, t1i = a + e, b + f, a - e, b - f
    t2r, t2i, t3r, t3i = c + g, d + h, c - g, d - h
    return [(t0r + t2r, t0i + t2i), (t1r + t3i, t1i - t3r), (t0r - t2r, t0i - t2i), (t1r - t3i, t1i + t3r)]


def dft8(x):
    r = np.float32(np.sqrt(0.5))
    even = [(x[i][0] + x[i + 4][0], x[i][1] + x[i + 4][1]) for i in range(4)]
    odd = [(x[i][0] - x[i + 4][0], x[i][1] - x[i + 4][1]) for i in range(4)]
    (p, q), (s, t), (u, v) = odd[1:]
    odd = [odd[0], ((p + q) * r, (q - p) * r), (t, -s), ((v - u) * r, -((u + v) * r))]
    out_even, out_odd = dft4(even), dft4(odd)
    return [out_even[0], out_odd[0], out_even[1], out_odd[1], out_even[2], out_odd[2], out_even[3], out_odd[3]]


def twiddle(value, power):
    re, im = value
    power %= GRID
    if power == 0:
        return value
    cos, sin = np.float32(np.cos(2 * np.pi * power / GRID)), np.float32(np.sin(2 * np.pi * power / GRID))
    return re * cos + im * sin, im * cos - re * sin


def dft64(src, dst, tmp, flip):
    first, second = (1, 0) if flip else (0, 1)
    for b in range(8):
        x = []
        for a in range(8):
            s, l = divmod(8 * a + b, BLOCK)
            x.append((src[s, l, first], src[s, l, second]))
        for k, value in enumerate(dft8(x)):
            re, im = twiddle(value, b * k)
            tmp[b, k, 0] = re
            tmp[b, k, 1] = im
    for k in range(8):
        out = dft8([(tmp[b, k, 0], tmp[b, k, 1]) for b in range(8)])
        for m, (re, im) in enumerate(out):
            s, l = divmod(k + 8 * m, BLOCK)
            dst[s, l, first] = re
            dst[s, l, second] = im


def block_transpose(x, lane):
    x = list(x)
    for bit in range(3):
        shift = BLOCK << bit
        low = (lane & shift) == 0
        for i in range(8):
            if i & (1 << bit) == 0:
                j = i | (1 << bit)
                a, b = x[i], x[j]
                x[i] = jnp.where(low, a, pltpu.roll(b, shift, 1))
                x[j] = jnp.where(low, pltpu.roll(a, 128 - shift, 1), b)
    return x


def kernel(rho_re, rho_im, g_re, g_im, w_first, w_z, w_back, w_last, phi, hat,
           in_re, in_im, sent, got, tmp, ga, gb, hat_stage, phi_stage,
           in_sem, hat_sem, phi_sem, own_sem, send_sem, recv_sem):
    fields = rho_re.shape[0]
    chunks = fields // GROUP
    units = 2 * chunks
    axis = ("py", "pz", "pz", "py")
    me = {name: lax.axis_index(name) for name in ("py", "pz")}

    barrier = pltpu.get_barrier_semaphore()
    for name in ("py", "pz"):
        for d in range(1, SIDE):
            pl.semaphore_signal(barrier, inc=1, device_id={name: lax.rem(me[name] + d, SIDE)}, device_id_type=MESH)

    def load(c):
        rows = pl.ds(c * GROUP, GROUP)
        return [pltpu.make_async_copy(rho.at[rows], buf.at[rows], in_sem.at[c, k])
                for k, (rho, buf) in enumerate(((rho_re, in_re), (rho_im, in_im)))]

    for c in range(chunks):
        for copy in load(c):
            copy.start()

    lane = lax.broadcasted_iota(jnp.int32, (8, 128), 1)

    def remote(phase, u, d):
        name = axis[phase]
        to = lax.rem(me[name] + d, SIDE)
        return pltpu.make_async_remote_copy(
            src_ref=sent.at[phase, u, to], dst_ref=got.at[phase, u, me[name]],
            send_sem=send_sem.at[phase, u, d - 1], recv_sem=recv_sem.at[phase, u, d - 1],
            device_id={name: to}, device_id_type=MESH)

    def own(phase, u):
        mine = me[axis[phase]]
        return pltpu.make_async_copy(sent.at[phase, u, mine], got.at[phase, u, mine], own_sem.at[phase, u])

    def send(phase, u):
        for d in (2, 1, 3) if axis[phase] == "pz" else (1, 3, 2):
            remote(phase, u, d).start()
        own(phase, u).start()

    def arrive(phase, u):
        for d in range(1, SIDE):
            remote(phase, u, d).wait_recv()
        own(phase, u).wait()

    def first_stage(c):
        for copy in load(c):
            copy.wait()

        def one(y, carry):
            rows = pl.ds(c * GROUP, GROUP)
            re = in_re[rows, y].reshape(GROUP * BLOCK, GRID)
            im = in_im[rows, y].reshape(GROUP * BLOCK, GRID)
            both = jnp.concatenate([re, im], axis=1)
            out = lax.dot_general(w_first[...], both, (((1,), (1,)), ((), ())), precision=HIGHEST,
                                  preferred_element_type=jnp.float32)
            out = out.reshape(2, SIDE, 2, HALF, 128)
            for h in range(2):
                for j in range(SIDE):
                    sent[0, 2 * c + h, j, y] = out[h, j]
            return carry

        lax.fori_loop(0, BLOCK, one, 0)

    def y_stage(u):
        arrive(0, u)
        dft64(got.at[0, u], sent.at[1, u], tmp, False)
        send(1, u)

    def hat_out(u):
        c, h = lax.div(u, 2), lax.rem(u, 2)
        return pltpu.make_async_copy(
            hat_stage.at[h],
            hat.at[pl.ds(c * GROUP, GROUP), pl.ds(h * (HALF * BLOCK), HALF * BLOCK)], hat_sem.at[h])

    STEP = 4

    def z_stage(u):
        h = lax.rem(u, 2)
        arrive(1, u)

        @pl.when(u >= 2)
        def _():
            hat_out(u - 2).wait()

        def one(step, carry):
            rows = []
            for i in range(STEP):
                ky = step * STEP + i
                rows += block_transpose([got[1, u, s, ky, c] for c in range(2) for s in range(SIDE)], lane)
            x = jnp.dot(jnp.concatenate(rows, axis=0), w_z[...], precision=HIGHEST,
                        preferred_element_type=jnp.float32)
            x = x.reshape(STEP, GROUP, HALF, 128)
            scaled = []
            for i in range(STEP):
                ky = step * STEP + i
                a, b = ga[h, ky], gb[h, ky]
                for f in range(GROUP):
                    v = x[i, f]
                    v = v * a + pltpu.roll(v, GRID, 1) * b
                    hat_stage[h, f, pl.ds(ky, HALF, stride=BLOCK), :] = v
                    scaled.append(v)
            x = jnp.dot(jnp.concatenate(scaled, axis=0), w_back[...], precision=HIGHEST,
                        preferred_element_type=jnp.float32)
            x = x.reshape(STEP, GROUP, HALF, 128)
            for i in range(STEP):
                ky = step * STEP + i
                out = block_transpose([x[i, f] for f in range(GROUP)], lane)
                for c in range(2):
                    for s in range(SIDE):
                        sent[2, u, s, ky, c] = out[c * SIDE + s]
            return carry

        lax.fori_loop(0, BLOCK // STEP, one, 0)
        send(2, u)
        hat_out(u).start()

    def back_y_stage(u):
        arrive(2, u)
        dft64(got.at[2, u], sent.at[3, u], tmp, True)
        send(3, u)

    def phi_out(c):
        slot = lax.rem(c, 2)
        return pltpu.make_async_copy(phi_stage.at[slot], phi.at[pl.ds(c * GROUP, GROUP)], phi_sem.at[slot])

    def last_stage(c):
        for h in range(2):
            arrive(3, 2 * c + h)
        slot = lax.rem(c, 2)

        @pl.when(c >= 2)
        def _():
            phi_out(c - 2).wait()

        def one(y, carry):
            x = jnp.concatenate([got[3, 2 * c + h, j, y].reshape(2 * HALF, 128)
                                 for h in range(2) for j in range(SIDE)], axis=0)
            out = lax.dot_general(x, w_last[...], (((0,), (0,)), ((), ())), precision=HIGHEST,
                                  preferred_element_type=jnp.float32)
            phi_stage[slot, :, pl.ds(pl.multiple_of(y * BLOCK, BLOCK), BLOCK), :] = out.reshape(GROUP, BLOCK, 128)
            return carry

        lax.fori_loop(0, BLOCK, one, 0)
        phi_out(c).start()

    for h in range(2):
        for ky in range(BLOCK):
            pick = pl.ds(h * HALF * BLOCK + ky, HALF, stride=BLOCK)
            re, im = g_re[pick, :], g_im[pick, :]
            ga[h, ky] = jnp.concatenate([re, re], axis=1)
            gb[h, ky] = jnp.concatenate([-im, im], axis=1)

    first_stage(0)
    pl.semaphore_wait(barrier, 2 * (SIDE - 1))
    send(0, 0)
    send(0, 1)

    def step(t, carry):
        @pl.when((lax.rem(t, 2) == 0) & (t // 2 + 1 < chunks))
        def _():
            c = lax.div(t, 2) + 1
            first_stage(c)
            send(0, 2 * c)
            send(0, 2 * c + 1)

        @pl.when(t < units)
        def _():
            y_stage(t)

        @pl.when((t >= 3) & (t < units + 3))
        def _():
            z_stage(t - 3)

        @pl.when((t >= 5) & (t < units + 5))
        def _():
            back_y_stage(t - 5)

        @pl.when((t >= 7) & (lax.rem(t, 2) == 1))
        def _():
            last_stage(lax.div(t - 7, 2))

        return carry

    lax.fori_loop(0, units + 6, step, 0)

    for u in range(units - 2, units):
        hat_out(u).wait()
    for c in range(chunks - 2, chunks):
        phi_out(c).wait()

    def finish(u, carry):
        for phase in range(4):
            for d in range(1, SIDE):
                remote(phase, u, d).wait_send()
        return carry

    lax.fori_loop(0, units, finish, 0)


def solve(rho_re, rho_im, g_re, g_im):
    fields = rho_re.shape[0]
    units = 2 * (fields // GROUP)
    f32 = jnp.float32
    vmem = pl.BlockSpec(memory_space=pltpu.VMEM)
    anywhere = pl.BlockSpec(memory_space=pl.ANY)
    weights = [jnp.asarray(t) for t in tables()]
    dma = pltpu.SemaphoreType.DMA
    phi, hat = pl.pallas_call(
        kernel,
        out_shape=[jax.ShapeDtypeStruct((fields, BLOCK * BLOCK, 128), f32)] * 2,
        in_specs=[anywhere] * 2 + [vmem] * 6,
        out_specs=[anywhere] * 2,
        scratch_shapes=[
            pltpu.VMEM((fields, BLOCK, BLOCK, GRID), f32),
            pltpu.VMEM((fields, BLOCK, BLOCK, GRID), f32),
            pltpu.VMEM((4, units, SIDE, BLOCK, 2, HALF, 128), f32),
            pltpu.VMEM((4, units, SIDE, BLOCK, 2, HALF, 128), f32),
            pltpu.VMEM((8, 8, 2, HALF, 128), f32),
            pltpu.VMEM((2, BLOCK, HALF, 128), f32),
            pltpu.VMEM((2, BLOCK, HALF, 128), f32),
            pltpu.VMEM((2, GROUP, HALF * BLOCK, 128), f32),
            pltpu.VMEM((2, GROUP, BLOCK * BLOCK, 128), f32),
            dma((fields // GROUP, 2)), dma((2,)), dma((2,)), dma((4, units)),
            dma((4, units, SIDE - 1)), dma((4, units, SIDE - 1)),
        ],
        compiler_params=pltpu.CompilerParams(collective_id=0, has_side_effects=True, vmem_limit_bytes=60 * 2**20),
        name="spectral_solve",
    )(jnp.transpose(rho_re, (0, 2, 3, 1)), jnp.transpose(rho_im, (0, 2, 3, 1)),
      g_re.reshape(BLOCK * BLOCK, GRID), g_im.reshape(BLOCK * BLOCK, GRID), *weights)
    phi = phi.reshape(fields, BLOCK, BLOCK, 128)
    hat = hat.reshape(fields, BLOCK, BLOCK, 128)
    phi_re = jnp.transpose(phi[..., :GRID], (0, 3, 1, 2))
    phi_im = jnp.transpose(phi[..., GRID:], (0, 3, 1, 2))
    return phi_re, phi_im, hat[..., :GRID], hat[..., GRID:]


def solution(mesh):
    space_layout = P("dp", None, "py", "pz")
    wave_layout = P("dp", "py", "pz", None)
    green_layout = P("py", "pz", None)
    return jax.shard_map(solve, mesh=mesh,
                         in_specs=(space_layout, space_layout, green_layout, green_layout),
                         out_specs=(space_layout, space_layout, wave_layout, wave_layout),
                         check_vma=False)
```

time: 861 us -> 226 us (0.26); the launches traced: 850 us -> 224 us
  local copies, waits for them, and re-layouts: 347 us -> 12.7 us
  Pallas kernels: 0 us -> 210 us
  blocking collectives: 153 us -> 0 us
  waiting for transfers between devices: 130 us -> 0 us
  matrix products: 126 us -> 0 us
  other arithmetic: 83.2 us -> 0 us
  starting transfers between devices: 10.5 us -> 0 us
    pallas_call x0 -> x1, Pallas kernels: none -> 210 us  [solve(): pl.pallas_call(kernel, out_shape=[jax.ShapeDtypeStruct((fields, BLOCK * B...]
    all_to_all x2 -> x0, blocking collectives: 153 us -> none  [regroup(): lax.all_to_all(halves, axis_name, split_dim + 1, concat_dim + 1, tiled=True)]
    all_to_all x2 -> x0, waiting for transfers between devices: 130 us -> none  [regroup(): lax.all_to_all(halves, axis_name, split_dim + 1, concat_dim + 1, tiled=True)]
    another operation x18 -> x0, matrix products: 126 us -> none  [the longest x3 44.6 us: local_solve(): jnp.fft.fft(volume, axis=3, norm='ortho') * lax.complex(g_re, g_im)]
    unnamed x38 -> x0, local copies, waits for them, and re-layouts: 121 us -> none
    slice x12 -> x0, local copies, waits for them, and re-layouts: 80.7 us -> none  [regroup(): return lax.complex(arrived[0], arrived[1])]
    another operation x4 -> x0, local copies, waits for them, and re-layouts: 64.8 us -> none  [regroup(): halves = jnp.stack([jnp.real(volume), jnp.imag(volume)])]
    all_to_all x4 -> x0, other arithmetic: 61.5 us -> none  [regroup(): lax.all_to_all(halves, axis_name, split_dim + 1, concat_dim + 1, tiled=True)]
  transfers between devices with their start and end apart: 2 -> 0, of which waited for: 2 -> 0; matrix products, arithmetic and copies ran while one was open for 1% -> 0% of each run, Pallas kernels for 0% -> 0%
where the time goes in v1:
time: 226 us; the launch traced here: 224 us
  Pallas kernels  210 us (93%)
  local copies, waits for them, and re-layouts  12.7 us (6%)
    pallas_call x1, Pallas kernels, solve(): pl.pallas_call(kernel, out_shape=[jax.ShapeDtypeStruct((fields, BLOCK * B...  210 us
    transpose x1, local copies, waits for them, and re-layouts, solve(): phi_im = jnp.transpose(phi[..., GRID:], (0, 3, 1, 2))  12.7 us

profile of v1, /device:TPU:0, one launch (start us, length us, event | category | flops | bytes accessed | tf_op | source)
XLA Modules:
  0.0 223.8 jit_solution(2895174953502626847)
XLA Ops:
  0.6 210.4 %spectral_solve.1 = (f32[32,256,128]{2,1,0:T(8,128)}, f32[32,256,128]{2,1,0:T(8,128)}) custom-call(f32[32,16,16,64]{3,2,1,0:T(8,128)} %bitcast.12, f32[32,16,16,64]{3,2,1,0:T(8,128)} %bitcast.13, f32[256,64]{1,0:T(8,128)} %bitcast.14, f32[256,64]{1,0:T(8,128)} %bitcast.15, f32[128,128]{1,0:T(8,128)} %constant.8.clone.w_first, f32[128,128]{1,0:T(8,128)} %constant.9.clone.w_z, ...), custom_call_target="tpu_custom_call" | custom-call | tf_op jit(solution)/shard_map/spectral_solve/pallas_call | solution.py:310
  211.1 12.7 %slice_bitcast_fusion = (f32[32,64,16,16]{1,3,2,0:T(8,128)}, f32[32,64,16,16]{1,3,2,0:T(8,128)}, f32[32,16,16,64]{3,2,1,0:T(8,128)}, f32[32,16,16,64]{3,2,1,0:T(8,128)}) fusion(f32[32,16,16,128]{3,2,1,0:T(8,128)} %bitcast.10, f32[32,16,16,128]{3,2,1,0:T(8,128)} %bitcast.11), kind=kLoop, calls=%fused_computation | loop fusion | bytes 16777216 | tf_op jit(solution)/shard_map/transpose | solution.py:335

commit v2 on v1

v2 whole, which is shorter than its diff:
```python
import jax
import jax.numpy as jnp
import numpy as np
from jax import lax
from jax.experimental import pallas as pl
from jax.experimental.pallas import tpu as pltpu
from jax.sharding import PartitionSpec as P

GRID = 64
SIDE = 4
BLOCK = 16
GROUP = 8
HALF = 8
HIGHEST = lax.Precision.HIGHEST
MESH = pl.DeviceIdType.MESH


def rotation(left, right, sign):
    angle = 2.0 * np.pi * (np.outer(left, right) % GRID) / GRID
    return np.cos(angle), sign * np.sin(angle)


def dft_matrix(rows_in, rows_out, sign, scale):
    cos, sin = rotation(rows_in, rows_out, sign)
    return np.block([[cos, sin], [-sin, cos]]) * scale


def tables():
    points = np.arange(GRID)
    kx = np.array([[[BLOCK * j + HALF * h + k for k in range(HALF)] for j in range(SIDE)] for h in range(2)])
    order = np.stack([kx, kx + GRID], axis=2).reshape(-1)
    first = dft_matrix(points, points, -1, 1.0 / 64).T[order]
    last = dft_matrix(points, points, 1, 1.0 / 8)[order]
    along_z = dft_matrix(points, points, -1, 1.0 / 8)
    back_z = dft_matrix(points, points, 1, 1.0 / 64)
    return [np.asarray(t, np.float32) for t in (first, along_z, back_z, last)]


def dft4(x):
    (a, b), (c, d), (e, f), (g, h) = x
    t0r, t0i, t1r, t1i = a + e, b + f, a - e, b - f
    t2r, t2i, t3r, t3i = c + g, d + h, c - g, d - h
    return [(t0r + t2r, t0i + t2i), (t1r + t3i, t1i - t3r), (t0r - t2r, t0i - t2i), (t1r - t3i, t1i + t3r)]


def dft8(x):
    r = np.float32(np.sqrt(0.5))
    even = [(x[i][0] + x[i + 4][0], x[i][1] + x[i + 4][1]) for i in range(4)]
    odd = [(x[i][0] - x[i + 4][0], x[i][1] - x[i + 4][1]) for i in range(4)]
    (p, q), (s, t), (u, v) = odd[1:]
    odd = [odd[0], ((p + q) * r, (q - p) * r), (t, -s), ((v - u) * r, -((u + v) * r))]
    out_even, out_odd = dft4(even), dft4(odd)
    return [out_even[0], out_odd[0], out_even[1], out_odd[1], out_even[2], out_odd[2], out_even[3], out_odd[3]]


def twiddle(value, power):
    re, im = value
    power %= GRID
    if power == 0:
        return value
    cos, sin = np.float32(np.cos(2 * np.pi * power / GRID)), np.float32(np.sin(2 * np.pi * power / GRID))
    return re * cos + im * sin, im * cos - re * sin


def dft64(src, dst, tmp, flip):
    first, second = (1, 0) if flip else (0, 1)
    for b in range(8):
        x = []
        for a in range(8):
            s, l = divmod(8 * a + b, BLOCK)
            x.append((src[s, l, first], src[s, l, second]))
        for k, value in enumerate(dft8(x)):
            re, im = twiddle(value, b * k)
            tmp[b, k, 0] = re
            tmp[b, k, 1] = im
    for k in range(8):
        out = dft8([(tmp[b, k, 0], tmp[b, k, 1]) for b in range(8)])
        for m, (re, im) in enumerate(out):
            s, l = divmod(k + 8 * m, BLOCK)
            dst[s, l, first] = re
            dst[s, l, second] = im


def block_transpose(x, lane):
    x = list(x)
    for bit in range(3):
        shift = BLOCK << bit
        low = (lane & shift) == 0
        for i in range(8):
            if i & (1 << bit) == 0:
                j = i | (1 << bit)
                a, b = x[i], x[j]
                x[i] = jnp.where(low, a, pltpu.roll(b, shift, 1))
                x[j] = jnp.where(low, pltpu.roll(a, 128 - shift, 1), b)
    return x


def kernel(rho_re, rho_im, g_re, g_im, w_first, w_z, w_back, w_last, phi_re, phi_im, hat_re, hat_im, last,
           in_re, in_im, sent, got, tmp, gv_re, gv_im, ga, gb, v_first, v_z, v_back, v_last,
           in_sem, small_sem, own_sem, send_sem, recv_sem):
    fields = rho_re.shape[0]
    chunks = fields // GROUP
    units = 2 * chunks
    axis = ("py", "pz", "pz", "py")
    me = {name: lax.axis_index(name) for name in ("py", "pz")}

    def load(c):
        rows = pl.ds(c * GROUP, GROUP)
        return [pltpu.make_async_copy(rho.at[rows], buf.at[rows], in_sem.at[c, k])
                for k, (rho, buf) in enumerate(((rho_re, in_re), (rho_im, in_im)))]

    small = [pltpu.make_async_copy(src, dst, small_sem.at[k]) for k, (src, dst) in enumerate(
        ((w_first, v_first), (w_z, v_z), (w_back, v_back), (w_last, v_last), (g_re, gv_re), (g_im, gv_im)))]

    small[0].start()
    for copy in load(0):
        copy.start()
    barrier = pltpu.get_barrier_semaphore()
    for name in ("py", "pz"):
        for d in range(1, SIDE):
            pl.semaphore_signal(barrier, inc=1, device_id={name: lax.rem(me[name] + d, SIDE)}, device_id_type=MESH)

    lane = lax.broadcasted_iota(jnp.int32, (8, 128), 1)

    def target(phase, u, slot):
        return last.at[u, slot] if phase == 3 else got.at[phase, u, slot]

    def remote(phase, u, d, part=None):
        name = axis[phase]
        to = lax.rem(me[name] + d, SIDE)
        src, dst = sent.at[phase, u, to], target(phase, u, me[name])
        if part is not None:
            src, dst = src.at[part], dst.at[part]
        return pltpu.make_async_remote_copy(
            src_ref=src, dst_ref=dst, send_sem=send_sem.at[phase, u, d - 1], recv_sem=recv_sem.at[phase, u, d - 1],
            device_id={name: to}, device_id_type=MESH)

    def own(phase, u):
        mine = me[axis[phase]]
        return pltpu.make_async_copy(sent.at[phase, u, mine], target(phase, u, mine), own_sem.at[phase, u])

    def send(phase, u):
        for d in (2, 1, 3) if axis[phase] == "pz" else (1, 3, 2):
            remote(phase, u, d).start()
        own(phase, u).start()

    def arrive(phase, u):
        for d in range(1, SIDE):
            remote(phase, u, d).wait_recv()
        own(phase, u).wait()

    def x_rows(c, part):
        def one(i, carry):
            for k in range(X_STEP):
                y = part * QUARTER + i * X_STEP + k
                rows = pl.ds(c * GROUP, GROUP)
                re = in_re[rows, y].reshape(GROUP * BLOCK, GRID)
                im = in_im[rows, y].reshape(GROUP * BLOCK, GRID)
                both = jnp.concatenate([re, im], axis=1)
                out = lax.dot_general(v_first[...], both, (((1,), (1,)), ((), ())), precision=HIGHEST,
                                      preferred_element_type=jnp.float32)
                out = out.reshape(2, SIDE, 2, HALF, 128)
                for h in range(2):
                    for j in range(SIDE):
                        sent[0, 2 * c + h, j, y] = out[h, j]
            return carry

        lax.fori_loop(0, QUARTER // X_STEP, one, 0)

    def first_stage(c):
        for copy in load(c):
            copy.wait()

        def quarter(part, carry):
            x_rows(c, part)
            for d in (1, 3, 2):
                remote(0, 2 * c, d, pl.ds(part * QUARTER, QUARTER)).start()
            return carry

        lax.fori_loop(0, BLOCK // QUARTER, quarter, 0)
        own(0, 2 * c).start()
        send(0, 2 * c + 1)

    def y_stage(u):
        arrive(0, u)
        dft64(got.at[0, u], sent.at[1, u], tmp, False)
        send(1, u)

    def z_stage(u):
        c, h = lax.div(u, 2), lax.rem(u, 2)
        arrive(1, u)

        def one(step, carry):
            rows = []
            for i in range(Z_STEP):
                ky = step * Z_STEP + i
                rows += block_transpose([got[1, u, s, ky, c] for c in range(2) for s in range(SIDE)], lane)
            x = jnp.dot(jnp.concatenate(rows, axis=0), v_z[...], precision=HIGHEST,
                        preferred_element_type=jnp.float32)
            x = x.reshape(Z_STEP, GROUP, HALF, 128)
            scaled = []
            for i in range(Z_STEP):
                ky = step * Z_STEP + i
                a, b = ga[h, ky], gb[h, ky]
                for f in range(GROUP):
                    v = x[i, f]
                    v = v * a + pltpu.roll(v, GRID, 1) * b
                    place = pl.ds(h * (HALF * BLOCK) + ky, HALF, stride=BLOCK)
                    hat_re[c * GROUP + f, place, :] = v[:, :GRID]
                    hat_im[c * GROUP + f, place, :] = pltpu.roll(v, GRID, 1)[:, :GRID]
                    scaled.append(v)
            x = jnp.dot(jnp.concatenate(scaled, axis=0), v_back[...], precision=HIGHEST,
                        preferred_element_type=jnp.float32)
            x = x.reshape(Z_STEP, GROUP, HALF, 128)
            for i in range(Z_STEP):
                ky = step * Z_STEP + i
                out = block_transpose([x[i, f] for f in range(GROUP)], lane)
                for part in range(2):
                    for s in range(SIDE):
                        sent[2, u, s, ky, part] = out[part * SIDE + s]
            return carry

        lax.fori_loop(0, BLOCK // Z_STEP, one, 0)
        send(2, u)

    def back_y_stage(u):
        arrive(2, u)
        dft64(got.at[2, u], sent.at[3, u], tmp, True)
        send(3, u)

    def last_stage(c):
        for h in range(2):
            arrive(3, 2 * c + h)
        back_x(last, 2 * c, v_last, phi_re, phi_im, c * GROUP)

    first = small[0]
    first.wait()
    pl.semaphore_wait(barrier, 2 * (SIDE - 1))
    first_stage(0)
    for c in range(1, chunks):
        for copy in load(c):
            copy.start()
    for copy in small[1:]:
        copy.start()
    for copy in small[1:]:
        copy.wait()

    def spread(ky, carry):
        for h in range(2):
            pick = pl.ds(h * HALF * BLOCK + ky, HALF, stride=BLOCK)
            re, im = gv_re[pick, :], gv_im[pick, :]
            ga[h, ky] = jnp.concatenate([re, re], axis=1)
            gb[h, ky] = jnp.concatenate([-im, im], axis=1)
        return carry

    lax.fori_loop(0, BLOCK, spread, 0)

    def step(t, carry):
        @pl.when((lax.rem(t, 2) == 0) & (t // 2 + 1 < chunks))
        def _():
            first_stage(lax.div(t, 2) + 1)

        @pl.when(t < units)
        def _():
            y_stage(t)

        @pl.when((t >= 3) & (t < units + 3))
        def _():
            z_stage(t - 3)

        @pl.when((t >= 5) & (t < units + 5))
        def _():
            back_y_stage(t - 5)

        @pl.when((t >= 7) & (lax.rem(t, 2) == 1))
        def _():
            last_stage(lax.div(t - 7, 2))

        return carry

    lax.fori_loop(0, units + 5, step, 0)
    for h in range(2):
        arrive(3, units - 2 + h)

    def finish(u, carry):
        for phase in range(4):
            for d in range(1, SIDE):
                remote(phase, u, d).wait_send()
        return carry

    lax.fori_loop(0, units, finish, 0)


def back_x(src, unit, table, out_re, out_im, start):
    def one(i, carry):
        for k in range(X_STEP):
            y = i * X_STEP + k
            x = jnp.concatenate([src[unit + h, j, y].reshape(2 * HALF, 128)
                                 for h in range(2) for j in range(SIDE)], axis=0)
            out = lax.dot_general(x, table[...], (((0,), (0,)), ((), ())), precision=HIGHEST,
                                  preferred_element_type=jnp.float32)
            place = pl.ds(pl.multiple_of(y * BLOCK, BLOCK), BLOCK)
            where = pl.ds(start, GROUP)
            out_re[where, place, :] = out[:, :GRID].reshape(GROUP, BLOCK, GRID)
            out_im[where, place, :] = pltpu.roll(out, GRID, 1)[:, :GRID].reshape(GROUP, BLOCK, GRID)
        return carry

    lax.fori_loop(0, BLOCK // X_STEP, one, 0)


def write_out(phi_re, phi_im, hat_re, hat_im, last, table, out_phi_re, out_phi_im, out_hat_re, out_hat_im,
              re, im, sem):
    done = phi_re.shape[0]
    copies = [pltpu.make_async_copy(src, dst, sem.at[k]) for k, (src, dst) in enumerate((
        (hat_re, out_hat_re), (hat_im, out_hat_im), (phi_re, out_phi_re.at[pl.ds(0, done)]),
        (phi_im, out_phi_im.at[pl.ds(0, done)])))]
    for copy in copies:
        copy.start()
    back_x(last, last.shape[0] - 2, table, re, im, 0)
    for k, (src, dst) in enumerate(((re, out_phi_re), (im, out_phi_im))):
        copies.append(pltpu.make_async_copy(src, dst.at[pl.ds(done, GROUP)], sem.at[4 + k]))
        copies[-1].start()
    for copy in copies:
        copy.wait()


QUARTER = 4
X_STEP = 2
Z_STEP = 4


def solve(rho_re, rho_im, g_re, g_im):
    fields = rho_re.shape[0]
    chunks = fields // GROUP
    units = 2 * chunks
    f32 = jnp.float32
    vmem = pl.BlockSpec(memory_space=pltpu.VMEM)
    anywhere = pl.BlockSpec(memory_space=pl.ANY)
    weights = [jnp.asarray(t) for t in tables()]
    dma = pltpu.SemaphoreType.DMA
    flat = BLOCK * BLOCK
    square = pltpu.VMEM((128, 128), f32)
    held = pl.pallas_call(
        kernel,
        out_shape=[pltpu.VMEM((fields - GROUP, flat, GRID), f32)] * 2 + [pltpu.VMEM((fields, flat, GRID), f32)] * 2
        + [pltpu.VMEM((units, SIDE, BLOCK, 2, HALF, 128), f32)],
        in_specs=[anywhere] * 8,
        out_specs=[vmem] * 5,
        scratch_shapes=[
            pltpu.VMEM((fields, BLOCK, BLOCK, GRID), f32),
            pltpu.VMEM((fields, BLOCK, BLOCK, GRID), f32),
            pltpu.VMEM((4, units, SIDE, BLOCK, 2, HALF, 128), f32),
            pltpu.VMEM((3, units, SIDE, BLOCK, 2, HALF, 128), f32),
            pltpu.VMEM((8, 8, 2, HALF, 128), f32),
            pltpu.VMEM((flat, GRID), f32),
            pltpu.VMEM((flat, GRID), f32),
            pltpu.VMEM((2, BLOCK, HALF, 128), f32),
            pltpu.VMEM((2, BLOCK, HALF, 128), f32),
            square, square, square, square,
            dma((chunks, 2)), dma((6,)), dma((4, units)),
            dma((4, units, SIDE - 1)), dma((4, units, SIDE - 1)),
        ],
        compiler_params=pltpu.CompilerParams(collective_id=0, has_side_effects=True, vmem_limit_bytes=41 * 2**20),
        name="spectral_solve",
    )(jnp.transpose(rho_re, (0, 2, 3, 1)), jnp.transpose(rho_im, (0, 2, 3, 1)),
      g_re.reshape(flat, GRID), g_im.reshape(flat, GRID), *weights)
    held = [pltpu.with_memory_space_constraint(x, pltpu.VMEM) for x in held]
    phi_re, phi_im, hat_re, hat_im = pl.pallas_call(
        write_out,
        out_shape=[jax.ShapeDtypeStruct((fields, flat, GRID), f32)] * 4,
        in_specs=[vmem] * 6,
        out_specs=[anywhere] * 4,
        scratch_shapes=[pltpu.VMEM((GROUP, flat, GRID), f32), pltpu.VMEM((GROUP, flat, GRID), f32), dma((6,))],
        compiler_params=pltpu.CompilerParams(vmem_limit_bytes=6 * 2**20),
        name="write_out",
    )(*held, weights[3])
    shape = (fields, BLOCK, BLOCK, GRID)
    phi_re = jnp.transpose(phi_re.reshape(shape), (0, 3, 1, 2))
    phi_im = jnp.transpose(phi_im.reshape(shape), (0, 3, 1, 2))
    return phi_re, phi_im, hat_re.reshape(shape), hat_im.reshape(shape)


def solution(mesh):
    space_layout = P("dp", None, "py", "pz")
    wave_layout = P("dp", "py", "pz", None)
    green_layout = P("py", "pz", None)
    return jax.shard_map(solve, mesh=mesh,
                         in_specs=(space_layout, space_layout, green_layout, green_layout),
                         out_specs=(space_layout, space_layout, wave_layout, wave_layout),
                         check_vma=False)
```

time: 226 us -> 213 us (0.942)
  local copies, waits for them, and re-layouts: 12.7 us -> 0.01 us
    transpose x1 -> x0, local copies, waits for them, and re-layouts: 12.7 us -> none  [solve(): phi_im = jnp.transpose(phi[..., GRID:], (0, 3, 1, 2))]
    pallas_call x1 -> x2, Pallas kernels: 210 us -> 211 us  [the longest x1 205 us: solve(): pl.pallas_call(kernel, out_shape=[pltpu.VMEM((fields - GROUP, flat, GRID)...]
where the time goes in v2:
time: 213 us; the launch traced here: 211 us
  Pallas kernels  211 us (99%)
    pallas_call x1, Pallas kernels, solve(): pl.pallas_call(kernel, out_shape=[pltpu.VMEM((fields - GROUP, flat, GRID)...  205 us
    pallas_call x1, Pallas kernels, solve(): pl.pallas_call(write_out, out_shape=[jax.ShapeDtypeStruct((fields, flat,...  5.87 us

profile of v2, /device:TPU:0, one launch (start us, length us, event | category | flops | bytes accessed | tf_op | source)
XLA Modules:
  0.0 211.4 jit_solution(1981134596526388908)
XLA Ops:
  0.6 0.0 copy-start
  0.6 204.8 %spectral_solve.1 = (f32[24,256,64]{2,1,0:T(8,128)S(1)}, f32[24,256,64]{2,1,0:T(8,128)S(1)}, f32[32,256,64]{2,1,0:T(8,128)S(1)}, f32[32,256,64]{2,1,0:T(8,128)S(1)}, f32[8,4,16,2,8,128]{5,4,3,2,1,0:T(8,128)S(1)}) custom-call(f32[32,16,16,64]{3,2,1,0:T(8,128)} %bitcast.12, f32[32,16,16,64]{3,2,1,0:T(8,128)} %bitcast.13, f32[256,64]{1,0:T(8,128)} %bitcast.14, ...), custom_call_target="tpu_custom_call" | custom-call | tf_op jit(solution)/shard_map/spectral_solve/pallas_call | solution.py:343
  205.5 0.0 copy-done
  205.5 5.9 %write_out.1 = (f32[32,256,64]{2,1,0:T(8,128)}, f32[32,256,64]{2,1,0:T(8,128)}, f32[32,256,64]{2,1,0:T(8,128)}, f32[32,256,64]{2,1,0:T(8,128)}) custom-call(f32[24,256,64]{2,1,0:T(8,128)S(1)} %get-tuple-element.13.phi_re, f32[24,256,64]{2,1,0:T(8,128)S(1)} %get-tuple-element.14.phi_im, f32[32,256,64]{2,1,0:T(8,128)S(1)} %get-tuple-element.15.hat_re, ...), custom_call_target="tpu_custom_call" | custom-call | tf_op jit(solution)/shard_map/write_out/pallas_call | solution.py:368
Async XLA Ops:
  0.6 204.8 %copy-start = (f32[128,128]{1,0:T(8,128)S(1)}, f32[128,128]{1,0:T(8,128)}, u32[]{:S(2)}) copy-start(f32[128,128]{1,0:T(8,128)} %constant.11.clone.w_last.table) | copy-start | bytes 196612

commit v3 on v2

--- a/solution.py
+++ b/solution.py
@@ -11,6 +11,7 @@
 BLOCK = 16
 GROUP = 8
 HALF = 8
+QUAD = 4
 HIGHEST = lax.Precision.HIGHEST
 MESH = pl.DeviceIdType.MESH
 
@@ -27,7 +28,7 @@
 
 def tables():
     points = np.arange(GRID)
-    kx = np.array([[[BLOCK * j + HALF * h + k for k in range(HALF)] for j in range(SIDE)] for h in range(2)])
+    kx = np.array([[[BLOCK * j + QUAD * q + k for k in range(QUAD)] for j in range(SIDE)] for q in range(QUAD)])
     order = np.stack([kx, kx + GRID], axis=2).reshape(-1)
     first = dft_matrix(points, points, -1, 1.0 / 64).T[order]
     last = dft_matrix(points, points, 1, 1.0 / 8)[order]
@@ -36,49 +37,42 @@
     return [np.asarray(t, np.float32) for t in (first, along_z, back_z, last)]
 
 
-def dft4(x):
-    (a, b), (c, d), (e, f), (g, h) = x
-    t0r, t0i, t1r, t1i = a + e, b + f, a - e, b - f
-    t2r, t2i, t3r, t3i = c + g, d + h, c - g, d - h
-    return [(t0r + t2r, t0i + t2i), (t1r + t3i, t1i - t3r), (t0r - t2r, t0i - t2i), (t1r - t3i, t1i + t3r)]
-
-
-def dft8(x):
+def dft4(x, turn):
+    even, odd = x[0] + x[2], x[0] - x[2]
+    both, side = x[1] + x[3], turn(x[1] - x[3])
+    return [even + both, odd + side, even - both, odd - side]
+
+
+def dft8(x, turn):
     r = np.float32(np.sqrt(0.5))
-    even = [(x[i][0] + x[i + 4][0], x[i][1] + x[i + 4][1]) for i in range(4)]
-    odd = [(x[i][0] - x[i + 4][0], x[i][1] - x[i + 4][1]) for i in range(4)]
-    (p, q), (s, t), (u, v) = odd[1:]
-    odd = [odd[0], ((p + q) * r, (q - p) * r), (t, -s), ((v - u) * r, -((u + v) * r))]
-    out_even, out_odd = dft4(even), dft4(odd)
-    return [out_even[0], out_odd[0], out_even[1], out_odd[1], out_even[2], out_odd[2], out_even[3], out_odd[3]]
-
-
-def twiddle(value, power):
-    re, im = value
-    power %= GRID
-    if power == 0:
-        return value
-    cos, sin = np.float32(np.cos(2 * np.pi * power / GRID)), np.float32(np.sin(2 * np.pi * power / GRID))
-    return re * cos + im * sin, im * cos - re * sin
-
-
-def dft64(src, dst, tmp, flip):
-    first, second = (1, 0) if flip else (0, 1)
+    even = [x[i] + x[i + 4] for i in range(4)]
+    odd = [x[i] - x[i + 4] for i in range(4)]
+    odd = [odd[0], (odd[1] + turn(odd[1])) * r, turn(odd[2]), (turn(odd[3]) - odd[3]) * r]
+    even, odd = dft4(even, turn), dft4(odd, turn)
+    return [value for pair in zip(even, odd) for value in pair]
+
+
+def dft64(src, dst, tmp, sign):
+    row = lax.broadcasted_iota(jnp.int32, (8, 128), 0)
+    signs = jnp.where(row < QUAD, np.float32(-sign), np.float32(sign))
+
+    def turn(value):
+        return pltpu.roll(value, QUAD, 0) * signs
+
+    def twiddle(value, power):
+        if power == 0:
+            return value
+        angle = 2 * np.pi * power / GRID
+        return value * np.float32(np.cos(angle)) + turn(value) * np.float32(np.sin(angle))
+
     for b in range(8):
-        x = []
-        for a in range(8):
-            s, l = divmod(8 * a + b, BLOCK)
-            x.append((src[s, l, first], src[s, l, second]))
-        for k, value in enumerate(dft8(x)):
-            re, im = twiddle(value, b * k)
-            tmp[b, k, 0] = re
-            tmp[b, k, 1] = im
+        x = [src[divmod(8 * a + b, BLOCK)] for a in range(8)]
+        for k, value in enumerate(dft8(x, turn)):
+            tmp[b, k] = twiddle(value, b * k)
     for k in range(8):
-        out = dft8([(tmp[b, k, 0], tmp[b, k, 1]) for b in range(8)])
-        for m, (re, im) in enumerate(out):
-            s, l = divmod(k + 8 * m, BLOCK)
-            dst[s, l, first] = re
-            dst[s, l, second] = im
+        out = dft8([tmp[b, k] for b in range(8)], turn)
+        for m, value in enumerate(out):
+            dst[divmod(k + 8 * m, BLOCK)] = value
 
 
 def block_transpose(x, lane):
@@ -100,7 +94,7 @@
            in_sem, small_sem, own_sem, send_sem, recv_sem):
     fields = rho_re.shape[0]
     chunks = fields // GROUP
-    units = 2 * chunks
+    units = QUAD * chunks
     axis = ("py", "pz", "pz", "py")
     me = {name: lax.axis_index(name) for name in ("py", "pz")}
 
@@ -121,6 +115,10 @@
             pl.semaphore_signal(barrier, inc=1, device_id={name: lax.rem(me[name] + d, SIDE)}, device_id_type=MESH)
 
     lane = lax.broadcasted_iota(jnp.int32, (8, 128), 1)
+    top = lax.broadcasted_iota(jnp.int32, (8, 128), 0) < QUAD
+
+    def swap(a, b):
+        return jnp.where(top, a, pltpu.roll(b, QUAD, 0)), jnp.where(top, pltpu.roll(a, QUAD, 0), b)
 
     def target(phase, u, slot):
         return last.at[u, slot] if phase == 3 else got.at[phase, u, slot]
@@ -159,42 +157,42 @@
                 both = jnp.concatenate([re, im], axis=1)
                 out = lax.dot_general(v_first[...], both, (((1,), (1,)), ((), ())), precision=HIGHEST,
                                       preferred_element_type=jnp.float32)
-                out = out.reshape(2, SIDE, 2, HALF, 128)
-                for h in range(2):
+                out = out.reshape(QUAD, SIDE, 2 * QUAD, 128)
+                for q in range(QUAD):
                     for j in range(SIDE):
-                        sent[0, 2 * c + h, j, y] = out[h, j]
+                        sent[0, QUAD * c + q, j, y] = out[q, j]
             return carry
 
         lax.fori_loop(0, QUARTER // X_STEP, one, 0)
 
     def first_stage(c):
-        for copy in load(c):
-            copy.wait()
-
         def quarter(part, carry):
             x_rows(c, part)
             for d in (1, 3, 2):
-                remote(0, 2 * c, d, pl.ds(part * QUARTER, QUARTER)).start()
+                remote(0, QUAD * c, d, pl.ds(part * QUARTER, QUARTER)).start()
             return carry
 
         lax.fori_loop(0, BLOCK // QUARTER, quarter, 0)
-        own(0, 2 * c).start()
-        send(0, 2 * c + 1)
+        own(0, QUAD * c).start()
+        for q in range(1, QUAD):
+            send(0, QUAD * c + q)
 
     def y_stage(u):
         arrive(0, u)
-        dft64(got.at[0, u], sent.at[1, u], tmp, False)
+        dft64(got.at[0, u], sent.at[1, u], tmp, -1)
         send(1, u)
 
     def z_stage(u):
         c, h = lax.div(u, 2), lax.rem(u, 2)
-        arrive(1, u)
+        for q in range(2):
+            arrive(1, 2 * u + q)
 
         def one(step, carry):
             rows = []
             for i in range(Z_STEP):
                 ky = step * Z_STEP + i
-                rows += block_transpose([got[1, u, s, ky, c] for c in range(2) for s in range(SIDE)], lane)
+                parts = [swap(got[1, 2 * u, s, ky], got[1, 2 * u + 1, s, ky]) for s in range(SIDE)]
+                rows += block_transpose([part[k] for k in range(2) for part in parts], lane)
             x = jnp.dot(jnp.concatenate(rows, axis=0), v_z[...], precision=HIGHEST,
                         preferred_element_type=jnp.float32)
             x = x.reshape(Z_STEP, GROUP, HALF, 128)
@@ -215,33 +213,34 @@
             for i in range(Z_STEP):
                 ky = step * Z_STEP + i
                 out = block_transpose([x[i, f] for f in range(GROUP)], lane)
-                for part in range(2):
-                    for s in range(SIDE):
-                        sent[2, u, s, ky, part] = out[part * SIDE + s]
+                for s in range(SIDE):
+                    sent[2, 2 * u, s, ky], sent[2, 2 * u + 1, s, ky] = swap(out[s], out[SIDE + s])
             return carry
 
         lax.fori_loop(0, BLOCK // Z_STEP, one, 0)
-        send(2, u)
+        for q in range(2):
+            send(2, 2 * u + q)
 
     def back_y_stage(u):
         arrive(2, u)
-        dft64(got.at[2, u], sent.at[3, u], tmp, True)
+        dft64(got.at[2, u], sent.at[3, u], tmp, 1)
         send(3, u)
 
     def last_stage(c):
-        for h in range(2):
-            arrive(3, 2 * c + h)
-        back_x(last, 2 * c, v_last, phi_re, phi_im, c * GROUP)
-
-    first = small[0]
-    first.wait()
-    pl.semaphore_wait(barrier, 2 * (SIDE - 1))
-    first_stage(0)
+        for q in range(QUAD):
+            arrive(3, QUAD * c + q)
+        back_x(last, QUAD * c, v_last, phi_re, phi_im, c * GROUP)
+
+    small[0].wait()
+    for copy in load(0):
+        copy.wait()
     for c in range(1, chunks):
         for copy in load(c):
             copy.start()
     for copy in small[1:]:
         copy.start()
+    pl.semaphore_wait(barrier, 2 * (SIDE - 1))
+    first_stage(0)
     for copy in small[1:]:
         copy.wait()
 
@@ -255,22 +254,27 @@
 
     lax.fori_loop(0, BLOCK, spread, 0)
 
+    pairs = units // 2
+
     def step(t, carry):
+        @pl.when(t < pairs)
+        def _():
+            lax.fori_loop(2 * t, 2 * t + 2, lambda u, k: (y_stage(u), k)[1], 0)
+
         @pl.when((lax.rem(t, 2) == 0) & (t // 2 + 1 < chunks))
         def _():
-            first_stage(lax.div(t, 2) + 1)
-
-        @pl.when(t < units)
-        def _():
-            y_stage(t)
-
-        @pl.when((t >= 3) & (t < units + 3))
+            c = lax.div(t, 2) + 1
+            for copy in load(c):
+                copy.wait()
+            first_stage(c)
+
+        @pl.when((t >= 3) & (t < pairs + 3))
         def _():
             z_stage(t - 3)
 
-        @pl.when((t >= 5) & (t < units + 5))
-        def _():
-            back_y_stage(t - 5)
+        @pl.when((t >= 5) & (t < pairs + 5))
+        def _():
+            lax.fori_loop(2 * (t - 5), 2 * (t - 5) + 2, lambda u, k: (back_y_stage(u), k)[1], 0)
 
         @pl.when((t >= 7) & (lax.rem(t, 2) == 1))
         def _():
@@ -278,9 +282,9 @@
 
         return carry
 
-    lax.fori_loop(0, units + 5, step, 0)
-    for h in range(2):
-        arrive(3, units - 2 + h)
+    lax.fori_loop(0, pairs + 5, step, 0)
+    for q in range(QUAD):
+        arrive(3, units - QUAD + q)
 
     def finish(u, carry):
         for phase in range(4):
@@ -295,8 +299,7 @@
     def one(i, carry):
         for k in range(X_STEP):
             y = i * X_STEP + k
-            x = jnp.concatenate([src[unit + h, j, y].reshape(2 * HALF, 128)
-                                 for h in range(2) for j in range(SIDE)], axis=0)
+            x = jnp.concatenate([src[unit + q, j, y] for q in range(QUAD) for j in range(SIDE)], axis=0)
             out = lax.dot_general(x, table[...], (((0,), (0,)), ((), ())), precision=HIGHEST,
                                   preferred_element_type=jnp.float32)
             place = pl.ds(pl.multiple_of(y * BLOCK, BLOCK), BLOCK)
@@ -316,7 +319,7 @@
         (phi_im, out_phi_im.at[pl.ds(0, done)])))]
     for copy in copies:
         copy.start()
-    back_x(last, last.shape[0] - 2, table, re, im, 0)
+    back_x(last, last.shape[0] - QUAD, table, re, im, 0)
     for k, (src, dst) in enumerate(((re, out_phi_re), (im, out_phi_im))):
         copies.append(pltpu.make_async_copy(src, dst.at[pl.ds(done, GROUP)], sem.at[4 + k]))
         copies[-1].start()
@@ -325,14 +328,14 @@
 
 
 QUARTER = 4
-X_STEP = 2
+X_STEP = 4
 Z_STEP = 4
 
 
 def solve(rho_re, rho_im, g_re, g_im):
     fields = rho_re.shape[0]
     chunks = fields // GROUP
-    units = 2 * chunks
+    units = QUAD * chunks
     f32 = jnp.float32
     vmem = pl.BlockSpec(memory_space=pltpu.VMEM)
     anywhere = pl.BlockSpec(memory_space=pl.ANY)
@@ -343,15 +346,15 @@
     held = pl.pallas_call(
         kernel,
         out_shape=[pltpu.VMEM((fields - GROUP, flat, GRID), f32)] * 2 + [pltpu.VMEM((fields, flat, GRID), f32)] * 2
-        + [pltpu.VMEM((units, SIDE, BLOCK, 2, HALF, 128), f32)],
+        + [pltpu.VMEM((units, SIDE, BLOCK, 2 * QUAD, 128), f32)],
         in_specs=[anywhere] * 8,
         out_specs=[vmem] * 5,
         scratch_shapes=[
             pltpu.VMEM((fields, BLOCK, BLOCK, GRID), f32),
             pltpu.VMEM((fields, BLOCK, BLOCK, GRID), f32),
-            pltpu.VMEM((4, units, SIDE, BLOCK, 2, HALF, 128), f32),
-            pltpu.VMEM((3, units, SIDE, BLOCK, 2, HALF, 128), f32),
-            pltpu.VMEM((8, 8, 2, HALF, 128), f32),
+            pltpu.VMEM((4, units, SIDE, BLOCK, 2 * QUAD, 128), f32),
+            pltpu.VMEM((3, units, SIDE, BLOCK, 2 * QUAD, 128), f32),
+            pltpu.VMEM((8, 8, 2 * QUAD, 128), f32),
             pltpu.VMEM((flat, GRID), f32),
             pltpu.VMEM((flat, GRID), f32),
             pltpu.VMEM((2, BLOCK, HALF, 128), f32),

time: 213 us -> 210 us (0.986)
  no operation moved by 1% of the time
where the time goes in v3:
time: 210 us
  Pallas kernels  209 us (100%)
    pallas_call x1, Pallas kernels, solve(): pl.pallas_call(kernel, out_shape=[pltpu.VMEM((fields - GROUP, flat, GRID)...  203 us
    pallas_call x1, Pallas kernels, solve(): pl.pallas_call(write_out, out_shape=[jax.ShapeDtypeStruct((fields, flat,...  5.87 us

profile of v3, /device:TPU:0, one launch (start us, length us, event | category | flops | bytes accessed | tf_op | source)
XLA Modules:
  0.0 209.8 jit_solution(17399442930063080576)
XLA Ops:
  0.6 0.0 copy-start
  0.6 203.3 %spectral_solve.1 = (f32[24,256,64]{2,1,0:T(8,128)S(1)}, f32[24,256,64]{2,1,0:T(8,128)S(1)}, f32[32,256,64]{2,1,0:T(8,128)S(1)}, f32[32,256,64]{2,1,0:T(8,128)S(1)}, f32[16,4,16,8,128]{4,3,2,1,0:T(8,128)S(1)}) custom-call(f32[32,16,16,64]{3,2,1,0:T(8,128)} %bitcast.12, f32[32,16,16,64]{3,2,1,0:T(8,128)} %bitcast.13, f32[256,64]{1,0:T(8,128)} %bitcast.14, ...), custom_call_target="tpu_custom_call" | custom-call | tf_op jit(solution)/shard_map/spectral_solve/pallas_call | solution.py:346
  203.9 0.0 copy-done
  203.9 5.9 %write_out.1 = (f32[32,256,64]{2,1,0:T(8,128)}, f32[32,256,64]{2,1,0:T(8,128)}, f32[32,256,64]{2,1,0:T(8,128)}, f32[32,256,64]{2,1,0:T(8,128)}) custom-call(f32[24,256,64]{2,1,0:T(8,128)S(1)} %get-tuple-element.13.phi_re, f32[24,256,64]{2,1,0:T(8,128)S(1)} %get-tuple-element.14.phi_im, f32[32,256,64]{2,1,0:T(8,128)S(1)} %get-tuple-element.15.hat_re, ...), custom_call_target="tpu_custom_call" | custom-call | tf_op jit(solution)/shard_map/write_out/pallas_call | solution.py:371
Async XLA Ops:
  0.6 203.3 %copy-start = (f32[128,128]{1,0:T(8,128)S(1)}, f32[128,128]{1,0:T(8,128)}, u32[]{:S(2)}) copy-start(f32[128,128]{1,0:T(8,128)} %constant.11.clone.w_last.table) | copy-start | bytes 196612

commit v4 on v3

--- a/solution.py
+++ b/solution.py
@@ -91,13 +91,23 @@
 
 def kernel(rho_re, rho_im, g_re, g_im, w_first, w_z, w_back, w_last, phi_re, phi_im, hat_re, hat_im, last,
            in_re, in_im, sent, got, tmp, gv_re, gv_im, ga, gb, v_first, v_z, v_back, v_last,
-           in_sem, small_sem, own_sem, send_sem, recv_sem):
+           part_sem, in_sem, small_sem, own_sem, send_sem, recv_sem):
     fields = rho_re.shape[0]
     chunks = fields // GROUP
     units = QUAD * chunks
     axis = ("py", "pz", "pz", "py")
     me = {name: lax.axis_index(name) for name in ("py", "pz")}
 
+    barrier = pltpu.get_barrier_semaphore()
+    for name in ("py", "pz"):
+        for d in range(1, SIDE):
+            pl.semaphore_signal(barrier, inc=1, device_id={name: lax.rem(me[name] + d, SIDE)}, device_id_type=MESH)
+
+    def load_part(part):
+        where = pl.ds(0, GROUP), pl.ds(part * QUARTER, QUARTER)
+        return [pltpu.make_async_copy(rho.at[where], buf.at[where], part_sem.at[part, k])
+                for k, (rho, buf) in enumerate(((rho_re, in_re), (rho_im, in_im)))]
+
     def load(c):
         rows = pl.ds(c * GROUP, GROUP)
         return [pltpu.make_async_copy(rho.at[rows], buf.at[rows], in_sem.at[c, k])
@@ -107,13 +117,9 @@
         ((w_first, v_first), (w_z, v_z), (w_back, v_back), (w_last, v_last), (g_re, gv_re), (g_im, gv_im)))]
 
     small[0].start()
-    for copy in load(0):
-        copy.start()
-    barrier = pltpu.get_barrier_semaphore()
-    for name in ("py", "pz"):
-        for d in range(1, SIDE):
-            pl.semaphore_signal(barrier, inc=1, device_id={name: lax.rem(me[name] + d, SIDE)}, device_id_type=MESH)
-
+    for part in range(BLOCK // QUARTER):
+        for copy in load_part(part):
+            copy.start()
     lane = lax.broadcasted_iota(jnp.int32, (8, 128), 1)
     top = lax.broadcasted_iota(jnp.int32, (8, 128), 0) < QUAD
 
@@ -149,33 +155,54 @@
 
     def x_rows(c, part):
         def one(i, carry):
+            rows = pl.ds(c * GROUP, GROUP)
+            start = part * QUARTER + i * X_STEP
+            both = []
             for k in range(X_STEP):
-                y = part * QUARTER + i * X_STEP + k
-                rows = pl.ds(c * GROUP, GROUP)
-                re = in_re[rows, y].reshape(GROUP * BLOCK, GRID)
-                im = in_im[rows, y].reshape(GROUP * BLOCK, GRID)
-                both = jnp.concatenate([re, im], axis=1)
-                out = lax.dot_general(v_first[...], both, (((1,), (1,)), ((), ())), precision=HIGHEST,
-                                      preferred_element_type=jnp.float32)
-                out = out.reshape(QUAD, SIDE, 2 * QUAD, 128)
+                re = in_re[rows, start + k].reshape(GROUP * BLOCK, GRID)
+                im = in_im[rows, start + k].reshape(GROUP * BLOCK, GRID)
+                both.append(jnp.concatenate([re, im], axis=1))
+            out = lax.dot_general(v_first[...], jnp.concatenate(both, axis=0), (((1,), (1,)), ((), ())),
+                                  precision=HIGHEST, preferred_element_type=jnp.float32)
+            out = out.reshape(QUAD, SIDE, 2 * QUAD, X_STEP * 128)
+            for k in range(X_STEP):
                 for q in range(QUAD):
                     for j in range(SIDE):
-                        sent[0, QUAD * c + q, j, y] = out[q, j]
+                        sent[0, QUAD * c + q, j, start + k] = out[q, j, :, k * 128:(k + 1) * 128]
             return carry
 
         lax.fori_loop(0, QUARTER // X_STEP, one, 0)
 
+    def send_part(part):
+        for d in (1, 3, 2):
+            remote(0, 0, d, pl.ds(part * QUARTER, QUARTER)).start()
+
     def first_stage(c):
+        lax.fori_loop(0, BLOCK // QUARTER, lambda part, k: (x_rows(c, part), k)[1], 0)
+        for q in range(QUAD):
+            send(0, QUAD * c + q)
+
+    def opening():
         def quarter(part, carry):
-            x_rows(c, part)
-            for d in (1, 3, 2):
-                remote(0, QUAD * c, d, pl.ds(part * QUARTER, QUARTER)).start()
+            for copy in load_part(part):
+                copy.wait()
+            x_rows(0, part)
+
+            @pl.when(part == 1)
+            def _():
+                pl.semaphore_wait(barrier, 2 * (SIDE - 1))
+                send_part(0)
+
+            @pl.when(part >= 1)
+            def _():
+                send_part(part)
+
             return carry
 
         lax.fori_loop(0, BLOCK // QUARTER, quarter, 0)
-        own(0, QUAD * c).start()
+        own(0, 0).start()
         for q in range(1, QUAD):
-            send(0, QUAD * c + q)
+            send(0, q)
 
     def y_stage(u):
         arrive(0, u)
@@ -231,16 +258,13 @@
             arrive(3, QUAD * c + q)
         back_x(last, QUAD * c, v_last, phi_re, phi_im, c * GROUP)
 
-    small[0].wait()
-    for copy in load(0):
-        copy.wait()
     for c in range(1, chunks):
         for copy in load(c):
             copy.start()
     for copy in small[1:]:
         copy.start()
-    pl.semaphore_wait(barrier, 2 * (SIDE - 1))
-    first_stage(0)
+    small[0].wait()
+    opening()
     for copy in small[1:]:
         copy.wait()
 
@@ -272,40 +296,46 @@
         def _():
             z_stage(t - 3)
 
-        @pl.when((t >= 5) & (t < pairs + 5))
+        @pl.when(t >= LAG)
         def _():
-            lax.fori_loop(2 * (t - 5), 2 * (t - 5) + 2, lambda u, k: (back_y_stage(u), k)[1], 0)
-
-        @pl.when((t >= 7) & (lax.rem(t, 2) == 1))
+            lax.fori_loop(2 * (t - LAG), 2 * (t - LAG) + 2, lambda u, k: (back_y_stage(u), k)[1], 0)
+
+        @pl.when((t >= LAG + 2) & (lax.rem(t - LAG, 2) == 0))
         def _():
-            last_stage(lax.div(t - 7, 2))
+            last_stage(lax.div(t - LAG, 2) - 1)
 
         return carry
 
-    lax.fori_loop(0, pairs + 5, step, 0)
+    lax.fori_loop(0, pairs + LAG, step, 0)
+
+    def sent_all(phase, first, end):
+        def one(u, carry):
+            for d in range(1, SIDE):
+                remote(phase, u, d).wait_send()
+            return carry
+
+        lax.fori_loop(first, end, one, 0)
+
+    for phase in range(3):
+        sent_all(phase, 0, units)
+    sent_all(3, 0, units - 2)
     for q in range(QUAD):
         arrive(3, units - QUAD + q)
-
-    def finish(u, carry):
-        for phase in range(4):
-            for d in range(1, SIDE):
-                remote(phase, u, d).wait_send()
-        return carry
-
-    lax.fori_loop(0, units, finish, 0)
+    sent_all(3, units - 2, units)
 
 
 def back_x(src, unit, table, out_re, out_im, start):
     def one(i, carry):
+        x = [jnp.concatenate([src[unit + q, j, i * X_STEP + k] for q in range(QUAD) for j in range(SIDE)], axis=0)
+             for k in range(X_STEP)]
+        out = lax.dot_general(jnp.concatenate(x, axis=1), table[...], (((0,), (0,)), ((), ())), precision=HIGHEST,
+                              preferred_element_type=jnp.float32)
+        where = pl.ds(start, GROUP)
         for k in range(X_STEP):
-            y = i * X_STEP + k
-            x = jnp.concatenate([src[unit + q, j, y] for q in range(QUAD) for j in range(SIDE)], axis=0)
-            out = lax.dot_general(x, table[...], (((0,), (0,)), ((), ())), precision=HIGHEST,
-                                  preferred_element_type=jnp.float32)
-            place = pl.ds(pl.multiple_of(y * BLOCK, BLOCK), BLOCK)
-            where = pl.ds(start, GROUP)
-            out_re[where, place, :] = out[:, :GRID].reshape(GROUP, BLOCK, GRID)
-            out_im[where, place, :] = pltpu.roll(out, GRID, 1)[:, :GRID].reshape(GROUP, BLOCK, GRID)
+            place = pl.ds(pl.multiple_of((i * X_STEP + k) * BLOCK, BLOCK), BLOCK)
+            part = out[k * 128:(k + 1) * 128]
+            out_re[where, place, :] = part[:, :GRID].reshape(GROUP, BLOCK, GRID)
+            out_im[where, place, :] = pltpu.roll(part, GRID, 1)[:, :GRID].reshape(GROUP, BLOCK, GRID)
         return carry
 
     lax.fori_loop(0, BLOCK // X_STEP, one, 0)
@@ -328,6 +358,7 @@
 
 
 QUARTER = 4
+LAG = 6
 X_STEP = 4
 Z_STEP = 4
 
@@ -360,7 +391,7 @@
             pltpu.VMEM((2, BLOCK, HALF, 128), f32),
             pltpu.VMEM((2, BLOCK, HALF, 128), f32),
             square, square, square, square,
-            dma((chunks, 2)), dma((6,)), dma((4, units)),
+            dma((BLOCK // QUARTER, 2)), dma((chunks, 2)), dma((6,)), dma((4, units)),
             dma((4, units, SIDE - 1)), dma((4, units, SIDE - 1)),
         ],
         compiler_params=pltpu.CompilerParams(collective_id=0, has_side_effects=True, vmem_limit_bytes=41 * 2**20),

time: 210 us -> 208 us (level)
    pallas_call x1, Pallas kernels: 203 us -> 201 us  [solve(): pl.pallas_call(kernel, out_shape=[pltpu.VMEM((fields - GROUP, flat, GRID)...]
where the time goes in v4:
time: 208 us
  Pallas kernels  207 us (100%)
    pallas_call x1, Pallas kernels, solve(): pl.pallas_call(kernel, out_shape=[pltpu.VMEM((fields - GROUP, flat, GRID)...  201 us
    pallas_call x1, Pallas kernels, solve(): pl.pallas_call(write_out, out_shape=[jax.ShapeDtypeStruct((fields, flat,...  5.87 us

profile of v4, /device:TPU:0, one launch (start us, length us, event | category | flops | bytes accessed | tf_op | source)
XLA Modules:
  0.0 207.7 jit_solution(15806761596733196991)
XLA Ops:
  0.6 0.0 copy-start
  0.6 201.1 %spectral_solve.1 = (f32[24,256,64]{2,1,0:T(8,128)S(1)}, f32[24,256,64]{2,1,0:T(8,128)S(1)}, f32[32,256,64]{2,1,0:T(8,128)S(1)}, f32[32,256,64]{2,1,0:T(8,128)S(1)}, f32[16,4,16,8,128]{4,3,2,1,0:T(8,128)S(1)}) custom-call(f32[32,16,16,64]{3,2,1,0:T(8,128)} %bitcast.12, f32[32,16,16,64]{3,2,1,0:T(8,128)} %bitcast.13, f32[256,64]{1,0:T(8,128)} %bitcast.14, ...), custom_call_target="tpu_custom_call" | custom-call | tf_op jit(solution)/shard_map/spectral_solve/pallas_call | solution.py:377
  201.8 0.0 copy-done
  201.8 5.9 %write_out.1 = (f32[32,256,64]{2,1,0:T(8,128)}, f32[32,256,64]{2,1,0:T(8,128)}, f32[32,256,64]{2,1,0:T(8,128)}, f32[32,256,64]{2,1,0:T(8,128)}) custom-call(f32[24,256,64]{2,1,0:T(8,128)S(1)} %get-tuple-element.13.phi_re, f32[24,256,64]{2,1,0:T(8,128)S(1)} %get-tuple-element.14.phi_im, f32[32,256,64]{2,1,0:T(8,128)S(1)} %get-tuple-element.15.hat_re, ...), custom_call_target="tpu_custom_call" | custom-call | tf_op jit(solution)/shard_map/write_out/pallas_call | solution.py:402
Async XLA Ops:
  0.6 201.1 %copy-start = (f32[128,128]{1,0:T(8,128)S(1)}, f32[128,128]{1,0:T(8,128)}, u32[]{:S(2)}) copy-start(f32[128,128]{1,0:T(8,128)} %constant.11.clone.w_last.table) | copy-start | bytes 196612

commit v5 on v4

--- a/solution.py
+++ b/solution.py
@@ -12,6 +12,7 @@
 GROUP = 8
 HALF = 8
 QUAD = 4
+PAIR = 2
 HIGHEST = lax.Precision.HIGHEST
 MESH = pl.DeviceIdType.MESH
 
@@ -28,8 +29,8 @@
 
 def tables():
     points = np.arange(GRID)
-    kx = np.array([[[BLOCK * j + QUAD * q + k for k in range(QUAD)] for j in range(SIDE)] for q in range(QUAD)])
-    order = np.stack([kx, kx + GRID], axis=2).reshape(-1)
+    q, j, h, c, k = np.ix_(range(QUAD), range(SIDE), range(2), range(2), range(PAIR))
+    order = (BLOCK * j + HALF * (q // 2) + PAIR * (q % 2) + QUAD * h + k + GRID * c).reshape(-1)
     first = dft_matrix(points, points, -1, 1.0 / 64).T[order]
     last = dft_matrix(points, points, 1, 1.0 / 8)[order]
     along_z = dft_matrix(points, points, -1, 1.0 / 8)
@@ -52,12 +53,16 @@
     return [value for pair in zip(even, odd) for value in pair]
 
 
+def real_rows():
+    return (lax.broadcasted_iota(jnp.int32, (8, 128), 0) & PAIR) == 0
+
+
 def dft64(src, dst, tmp, sign):
-    row = lax.broadcasted_iota(jnp.int32, (8, 128), 0)
-    signs = jnp.where(row < QUAD, np.float32(-sign), np.float32(sign))
+    real = real_rows()
+    signs = jnp.where(real, np.float32(-sign), np.float32(sign))
 
     def turn(value):
-        return pltpu.roll(value, QUAD, 0) * signs
+        return jnp.where(real, pltpu.roll(value, 8 - PAIR, 0), pltpu.roll(value, PAIR, 0)) * signs
 
     def twiddle(value, power):
         if power == 0:
@@ -90,8 +95,9 @@
 
 
 def kernel(rho_re, rho_im, g_re, g_im, w_first, w_z, w_back, w_last, phi_re, phi_im, hat_re, hat_im, last,
-           in_re, in_im, sent, got, tmp, gv_re, gv_im, ga, gb, v_first, v_z, v_back, v_last,
-           part_sem, in_sem, small_sem, own_sem, send_sem, recv_sem):
+           in_re, in_im, sent, got, half_got, half_sent, tmp, gv_re, gv_im, ga, gb, v_first, v_z, v_back, v_last,
+           part_sem, in_sem, small_sem, own_sem, send_sem, recv_sem,
+           half_own_sem, half_send_sem, half_recv_sem):
     fields = rho_re.shape[0]
     chunks = fields // GROUP
     units = QUAD * chunks
@@ -121,10 +127,10 @@
         for copy in load_part(part):
             copy.start()
     lane = lax.broadcasted_iota(jnp.int32, (8, 128), 1)
-    top = lax.broadcasted_iota(jnp.int32, (8, 128), 0) < QUAD
+    real = real_rows()
 
     def swap(a, b):
-        return jnp.where(top, a, pltpu.roll(b, QUAD, 0)), jnp.where(top, pltpu.roll(a, QUAD, 0), b)
+        return jnp.where(real, a, pltpu.roll(b, PAIR, 0)), jnp.where(real, pltpu.roll(a, 8 - PAIR, 0), b)
 
     def target(phase, u, slot):
         return last.at[u, slot] if phase == 3 else got.at[phase, u, slot]
@@ -142,6 +148,58 @@
     def own(phase, u):
         mine = me[axis[phase]]
         return pltpu.make_async_copy(sent.at[phase, u, mine], target(phase, u, mine), own_sem.at[phase, u])
+
+    def half_ends(phase, h, to, mine):
+        if phase == 0:
+            return sent.at[0, 0, to], half_got.at[0, h, mine]
+        if phase == 1:
+            return half_sent.at[0, h, to], got.at[1, 0, mine]
+        if phase == 2:
+            return sent.at[2, units - 1, to], half_got.at[1, h, mine]
+        return half_sent.at[1, h, to], last.at[units - 1, mine]
+
+    def remote_half(phase, h, d, part=None):
+        name = axis[phase]
+        to = lax.rem(me[name] + d, SIDE)
+        where = pl.ds(0, BLOCK) if part is None else part, pl.ds(QUAD * h, QUAD)
+        src, dst = half_ends(phase, h, to, me[name])
+        return pltpu.make_async_remote_copy(
+            src_ref=src.at[where], dst_ref=dst.at[where],
+            send_sem=half_send_sem.at[phase, h, d - 1], recv_sem=half_recv_sem.at[phase, h, d - 1],
+            device_id={name: to}, device_id_type=MESH)
+
+    def own_half(phase, h):
+        mine = me[axis[phase]]
+        where = pl.ds(0, BLOCK), pl.ds(QUAD * h, QUAD)
+        src, dst = half_ends(phase, h, mine, mine)
+        return pltpu.make_async_copy(src.at[where], dst.at[where], half_own_sem.at[phase, h])
+
+    def send_half(phase, h):
+        for d in (2, 1, 3) if axis[phase] == "pz" else (1, 3, 2):
+            remote_half(phase, h, d).start()
+        own_half(phase, h).start()
+
+    def arrive_half(phase, h):
+        for d in range(1, SIDE):
+            remote_half(phase, h, d).wait_recv()
+        own_half(phase, h).wait()
+
+    def half_y_stage(phase, sign):
+        def one(h, carry):
+            for k in range(2):
+                @pl.when(h == k)
+                def _():
+                    arrive_half(phase, k)
+
+            dft64(half_got.at[phase // 2, h], half_sent.at[phase // 2, h], tmp, sign)
+            for k in range(2):
+                @pl.when(h == k)
+                def _():
+                    send_half(phase + 1, k)
+
+            return carry
+
+        lax.fori_loop(0, 2, one, 0)
 
     def send(phase, u):
         for d in (2, 1, 3) if axis[phase] == "pz" else (1, 3, 2):
@@ -175,7 +233,7 @@
 
     def send_part(part):
         for d in (1, 3, 2):
-            remote(0, 0, d, pl.ds(part * QUARTER, QUARTER)).start()
+            remote_half(0, 0, d, pl.ds(part * QUARTER, QUARTER)).start()
 
     def first_stage(c):
         lax.fori_loop(0, BLOCK // QUARTER, lambda part, k: (x_rows(c, part), k)[1], 0)
@@ -200,19 +258,30 @@
             return carry
 
         lax.fori_loop(0, BLOCK // QUARTER, quarter, 0)
-        own(0, 0).start()
+        own_half(0, 0).start()
+        send_half(0, 1)
         for q in range(1, QUAD):
             send(0, q)
 
     def y_stage(u):
-        arrive(0, u)
-        dft64(got.at[0, u], sent.at[1, u], tmp, -1)
-        send(1, u)
+        @pl.when(u > 0)
+        def _():
+            arrive(0, u)
+            dft64(got.at[0, u], sent.at[1, u], tmp, -1)
+            send(1, u)
 
     def z_stage(u):
         c, h = lax.div(u, 2), lax.rem(u, 2)
-        for q in range(2):
-            arrive(1, 2 * u + q)
+        @pl.when(u == 0)
+        def _():
+            for h in range(2):
+                arrive_half(1, h)
+
+        @pl.when(u > 0)
+        def _():
+            arrive(1, 2 * u)
+
+        arrive(1, 2 * u + 1)
 
         def one(step, carry):
             rows = []
@@ -245,13 +314,23 @@
             return carry
 
         lax.fori_loop(0, BLOCK // Z_STEP, one, 0)
-        for q in range(2):
-            send(2, 2 * u + q)
+        send(2, 2 * u)
+
+        @pl.when(2 * u + 2 < units)
+        def _():
+            send(2, 2 * u + 1)
+
+        @pl.when(2 * u + 2 == units)
+        def _():
+            for h in range(2):
+                send_half(2, h)
 
     def back_y_stage(u):
-        arrive(2, u)
-        dft64(got.at[2, u], sent.at[3, u], tmp, 1)
-        send(3, u)
+        @pl.when(u + 1 < units)
+        def _():
+            arrive(2, u)
+            dft64(got.at[2, u], sent.at[3, u], tmp, 1)
+            send(3, u)
 
     def last_stage(c):
         for q in range(QUAD):
@@ -277,6 +356,7 @@
         return carry
 
     lax.fori_loop(0, BLOCK, spread, 0)
+    half_y_stage(0, -1)
 
     pairs = units // 2
 
@@ -316,12 +396,18 @@
 
         lax.fori_loop(first, end, one, 0)
 
-    for phase in range(3):
-        sent_all(phase, 0, units)
-    sent_all(3, 0, units - 2)
-    for q in range(QUAD):
+    half_y_stage(2, 1)
+    for phase, first, end in ((0, 1, units), (1, 1, units), (2, 0, units - 1), (3, 0, units - 2)):
+        sent_all(phase, first, end)
+    for q in range(QUAD - 1):
         arrive(3, units - QUAD + q)
-    sent_all(3, units - 2, units)
+    for h in range(2):
+        arrive_half(3, h)
+    sent_all(3, units - 2, units - 1)
+    for phase in range(4):
+        for h in range(2):
+            for d in range(1, SIDE):
+                remote_half(phase, h, d).wait_send()
 
 
 def back_x(src, unit, table, out_re, out_im, start):
@@ -385,6 +471,8 @@
             pltpu.VMEM((fields, BLOCK, BLOCK, GRID), f32),
             pltpu.VMEM((4, units, SIDE, BLOCK, 2 * QUAD, 128), f32),
             pltpu.VMEM((3, units, SIDE, BLOCK, 2 * QUAD, 128), f32),
+            pltpu.VMEM((2, 2, SIDE, BLOCK, 2 * QUAD, 128), f32),
+            pltpu.VMEM((2, 2, SIDE, BLOCK, 2 * QUAD, 128), f32),
             pltpu.VMEM((8, 8, 2 * QUAD, 128), f32),
             pltpu.VMEM((flat, GRID), f32),
             pltpu.VMEM((flat, GRID), f32),
@@ -393,6 +481,7 @@
             square, square, square, square,
             dma((BLOCK // QUARTER, 2)), dma((chunks, 2)), dma((6,)), dma((4, units)),
             dma((4, units, SIDE - 1)), dma((4, units, SIDE - 1)),
+            dma((4, 2)), dma((4, 2, SIDE - 1)), dma((4, 2, SIDE - 1)),
         ],
         compiler_params=pltpu.CompilerParams(collective_id=0, has_side_effects=True, vmem_limit_bytes=41 * 2**20),
         name="spectral_solve",

time: 208 us -> 207 us (level)
  no operation moved by 1% of the time
where the time goes in v5:
time: 207 us
  Pallas kernels  206 us (100%)
    pallas_call x1, Pallas kernels, solve(): pl.pallas_call(kernel, out_shape=[pltpu.VMEM((fields - GROUP, flat, GRID)...  200 us
    pallas_call x1, Pallas kernels, solve(): pl.pallas_call(write_out, out_shape=[jax.ShapeDtypeStruct((fields, flat,...  5.87 us

profile of v5, /device:TPU:0, one launch (start us, length us, event | category | flops | bytes accessed | tf_op | source)
XLA Modules:
  0.0 206.9 jit_solution(13609263925719583967)
XLA Ops:
  0.6 0.0 copy-start
  0.6 200.3 %spectral_solve.1 = (f32[24,256,64]{2,1,0:T(8,128)S(1)}, f32[24,256,64]{2,1,0:T(8,128)S(1)}, f32[32,256,64]{2,1,0:T(8,128)S(1)}, f32[32,256,64]{2,1,0:T(8,128)S(1)}, f32[16,4,16,8,128]{4,3,2,1,0:T(8,128)S(1)}) custom-call(f32[32,16,16,64]{3,2,1,0:T(8,128)} %bitcast.12, f32[32,16,16,64]{3,2,1,0:T(8,128)} %bitcast.13, f32[256,64]{1,0:T(8,128)} %bitcast.14, ...), custom_call_target="tpu_custom_call" | custom-call | tf_op jit(solution)/shard_map/spectral_solve/pallas_call | solution.py:463
  201.0 0.0 copy-done
  201.0 5.9 %write_out.1 = (f32[32,256,64]{2,1,0:T(8,128)}, f32[32,256,64]{2,1,0:T(8,128)}, f32[32,256,64]{2,1,0:T(8,128)}, f32[32,256,64]{2,1,0:T(8,128)}) custom-call(f32[24,256,64]{2,1,0:T(8,128)S(1)} %get-tuple-element.13.phi_re, f32[24,256,64]{2,1,0:T(8,128)S(1)} %get-tuple-element.14.phi_im, f32[32,256,64]{2,1,0:T(8,128)S(1)} %get-tuple-element.15.hat_re, ...), custom_call_target="tpu_custom_call" | custom-call | tf_op jit(solution)/shard_map/write_out/pallas_call | solution.py:491
Async XLA Ops:
  0.6 200.3 %copy-start = (f32[128,128]{1,0:T(8,128)S(1)}, f32[128,128]{1,0:T(8,128)}, u32[]{:S(2)}) copy-start(f32[128,128]{1,0:T(8,128)} %constant.11.clone.w_last.table) | copy-start | bytes 196612

commit v6 on v5

--- a/solution.py
+++ b/solution.py
@@ -246,15 +246,11 @@
                 copy.wait()
             x_rows(0, part)
 
-            @pl.when(part == 1)
+            @pl.when(part == 0)
             def _():
                 pl.semaphore_wait(barrier, 2 * (SIDE - 1))
-                send_part(0)
-
-            @pl.when(part >= 1)
-            def _():
-                send_part(part)
-
+
+            send_part(part)
             return carry
 
         lax.fori_loop(0, BLOCK // QUARTER, quarter, 0)
@@ -372,9 +368,9 @@
                 copy.wait()
             first_stage(c)
 
-        @pl.when((t >= 3) & (t < pairs + 3))
-        def _():
-            z_stage(t - 3)
+        @pl.when((t >= 7) & (t < pairs + 7))
+        def _():
+            z_stage(t - 7)
 
         @pl.when(t >= LAG)
         def _():
@@ -444,7 +440,7 @@
 
 
 QUARTER = 4
-LAG = 6
+LAG = 13
 X_STEP = 4
 Z_STEP = 4
 

time: 207 us -> 207 us (level)
  no operation moved by 1% of the time
where the time goes in v6:
time: 207 us
  Pallas kernels  206 us (100%)
    pallas_call x1, Pallas kernels, solve(): pl.pallas_call(kernel, out_shape=[pltpu.VMEM((fields - GROUP, flat, GRID)...  200 us
    pallas_call x1, Pallas kernels, solve(): pl.pallas_call(write_out, out_shape=[jax.ShapeDtypeStruct((fields, flat,...  5.87 us

profile of v6, /device:TPU:0, one launch (start us, length us, event | category | flops | bytes accessed | tf_op | source)
XLA Modules:
  0.0 206.7 jit_solution(13076709712203634680)
XLA Ops:
  0.6 0.0 copy-start
  0.6 200.2 %spectral_solve.1 = (f32[24,256,64]{2,1,0:T(8,128)S(1)}, f32[24,256,64]{2,1,0:T(8,128)S(1)}, f32[32,256,64]{2,1,0:T(8,128)S(1)}, f32[32,256,64]{2,1,0:T(8,128)S(1)}, f32[16,4,16,8,128]{4,3,2,1,0:T(8,128)S(1)}) custom-call(f32[32,16,16,64]{3,2,1,0:T(8,128)} %bitcast.12, f32[32,16,16,64]{3,2,1,0:T(8,128)} %bitcast.13, f32[256,64]{1,0:T(8,128)} %bitcast.14, ...), custom_call_target="tpu_custom_call" | custom-call | tf_op jit(solution)/shard_map/spectral_solve/pallas_call | solution.py:459
  200.8 0.0 copy-done
  200.8 5.9 %write_out.1 = (f32[32,256,64]{2,1,0:T(8,128)}, f32[32,256,64]{2,1,0:T(8,128)}, f32[32,256,64]{2,1,0:T(8,128)}, f32[32,256,64]{2,1,0:T(8,128)}) custom-call(f32[24,256,64]{2,1,0:T(8,128)S(1)} %get-tuple-element.13.phi_re, f32[24,256,64]{2,1,0:T(8,128)S(1)} %get-tuple-element.14.phi_im, f32[32,256,64]{2,1,0:T(8,128)S(1)} %get-tuple-element.15.hat_re, ...), custom_call_target="tpu_custom_call" | custom-call | tf_op jit(solution)/shard_map/write_out/pallas_call | solution.py:487
Async XLA Ops:
  0.6 200.2 %copy-start = (f32[128,128]{1,0:T(8,128)S(1)}, f32[128,128]{1,0:T(8,128)}, u32[]{:S(2)}) copy-start(f32[128,128]{1,0:T(8,128)} %constant.11.clone.w_last.table) | copy-start | bytes 196612
